TPU v7x, 32 devices: a whole 2x2x4 slice. The times are simulated.
32 devices in a mesh: shift: 16 (over z, x, core), row: 2 (over y).
Axes of the slice: x: 2, y: 2, z: 4, core: 2. Of those that a mesh axis runs over, the one named last changes fastest.
Arguments:
- solutions: bfloat16 [32, 2, 2048, 128], P('shift', None, 'row'), may hold values from -96 to 96
Outputs:
- moments: bfloat16 [2, 8, 2048, 128], P(None, None, ('row', 'shift'))
- gram_real: float32 [1024, 1024], replicated
- gram_imag: float32 [1024, 1024], replicated
All inputs are finite; a program needn't handle non-finite values.
Results may differ from a plain program's by a relative error of at most 0.0061.
Values may be sent and summed in bfloat16 or wider, within the bound.
A program may use at most 64 MiB of HBM per device.

v0:
```python
import math

import jax
import jax.numpy as jnp
from jax import lax
from jax.sharding import PartitionSpec as P

PANELS = 8


def coefficient_block(first_shift, shift_count, all_shifts, panels):
    indices = (first_shift + jnp.arange(shift_count, dtype=jnp.int32)).astype(jnp.float32)
    orders = jnp.arange(1, panels + 1, dtype=jnp.int32).astype(jnp.float32)
    angles = orders[:, None] * (2.0 * math.pi * (indices + 0.5) / all_shifts)[None, :]
    cos_part = jnp.cos(angles) / all_shifts
    sin_part = jnp.sin(angles) / all_shifts
    real_row = jnp.stack([cos_part, -sin_part], axis=-1)
    imag_row = jnp.stack([sin_part, cos_part], axis=-1)
    return (
        jnp.stack([real_row, imag_row], axis=0)
        .reshape(2 * panels, 2 * shift_count)
        .astype(jnp.bfloat16)
    )


def weigh(block_data, first_shift, all_shifts):
    shift_count = block_data.shape[0]
    weights = coefficient_block(first_shift, shift_count, all_shifts, PANELS)
    flat = block_data.reshape(2 * shift_count, -1)
    product = jnp.dot(weights, flat, preferred_element_type=jnp.float32)
    return product.reshape(2, PANELS, block_data.shape[2], block_data.shape[3])


def pair_product(left, right):
    width = left.shape[0] * left.shape[2]
    return jnp.einsum("krl,qrm->klqm", left, right, preferred_element_type=jnp.float32).reshape(
        width, width
    )


def gram_terms(moment_block):
    real_part = moment_block[0]
    imag_part = moment_block[1]
    gram_real = pair_product(real_part, real_part) + pair_product(imag_part, imag_part)
    gram_imag = pair_product(real_part, imag_part) - pair_product(imag_part, real_part)
    return (gram_real, gram_imag)


def local(solutions):
    shift_count = solutions.shape[0]
    all_shifts = shift_count * lax.axis_size("shift")
    moment_sum = weigh(
        lax.all_to_all(solutions, "shift", split_axis=2, concat_axis=0, tiled=True), 0, all_shifts
    )
    moments = moment_sum.astype(jnp.bfloat16)
    row_count = moments.shape[2] * lax.axis_size("shift") * lax.axis_size("row")
    shard_real, shard_imag = gram_terms(moments)
    gram_real, gram_imag = lax.psum((shard_real, shard_imag), ("shift", "row"))
    factor = 1.0 / math.sqrt(row_count)
    return (moments, gram_real * factor, gram_imag * factor)


def solution(mesh):
    placed = (P("shift", None, "row", None),)
    return jax.shard_map(
        local,
        mesh=mesh,
        in_specs=placed,
        out_specs=(P(None, None, ("row", "shift"), None), P(), P()),
        check_vma=False,
    )
```

profile of v0, /device:TPU:1, one launch (start us, length us, event | category | flops | bytes accessed | tf_op | source)
XLA Modules:
  0.0 244.9 jit_solution(16448146008260359767)
XLA Ops:
  7.2 3.3 %copy.14 = bf16[2,2,1024,128]{3,1,0,2:T(2,128)(2,1)} copy(bf16[2,2,1024,128]{3,2,1,0:T(8,128)(2,1)} %param.1) | data formatting | bytes 2097152 | tf_op args[0]
  10.4 7.3 %all-to-all-start = ((bf16[2,2,1024,128]{3,1,0,2:T(2,128)(2,1)}), bf16[2,2,1024,128]{3,1,0,2:T(2,128)(2,1)S(1)}, u32[]{:S(2)}, u32[]{:S(2)}) async-start(bf16[2,2,1024,128]{3,1,0,2:T(2,128)(2,1)} %copy.14), calls=%async_computation | async-start | bytes 2097152 | tf_op jit(solution)/shard_map/all_to_all | solution.py:53
  17.7 0.0 all-reduce.3.cloned.1.call-start
  17.8 0.1 fusion.20
  17.9 0.1 copy.10
  18.0 0.1 copy.12
  18.1 0.1 copy.11
  18.2 0.1 copy.13
  18.3 22.6 %all-to-all-done = bf16[2,2,1024,128]{3,1,0,2:T(2,128)(2,1)S(1)} async-done(((bf16[2,2,1024,128]{3,1,0,2:T(2,128)(2,1)}), bf16[2,2,1024,128]{3,1,0,2:T(2,128)(2,1)S(1)}, u32[]{:S(2)}, u32[]{:S(2)}) %all-to-all-start) | async-done | bytes 1048608 | tf_op jit(solution)/shard_map/all_to_all | solution.py:53
  40.9 0.3 copy.15
  41.2 0.7 convolution_convert_fusion
  41.9 0.7 fusion.7
  42.6 0.7 fusion.2
  43.4 2.8 %convolution_subtract_fusion = f32[1024,1024]{1,0:T(8,128)} fusion(f32[1024,1024]{1,0:T(8,128)S(1)} %fusion.2, bf16[8,8,8,128]{3,2,1,0:T(8,128)(2,1)S(1)} %bitcast.54, bf16[8,8,8,128]{3,2,1,0:T(8,128)(2,1)S(1)} %bitcast.58), kind=kOutput, calls=%fused_computation | convolution fusion | flops 135266304 | bytes 8650752 | tf_op jit(solution)/shard_map/krl,qrm->klqm/dot_general | solution.py:36
  46.1 2.7 %convolution_add_fusion = f32[1024,1024]{1,0:T(8,128)} fusion(f32[1024,1024]{1,0:T(8,128)S(1)} %fusion.7, bf16[8,8,8,128]{3,2,1,0:T(8,128)(2,1)S(1)} %bitcast.55), kind=kOutput, calls=%fused_computation.1 | convolution fusion | flops 135266304 | bytes 8519680 | tf_op jit(solution)/shard_map/krl,qrm->klqm/dot_general | solution.py:36
  48.9 0.0 all-reduce.3.cloned.1.call-update
  48.9 0.8 copy.17
  49.6 179.5 %all-reduce.3.cloned.1.call-done = (f32[1024,1024]{1,0:T(8,128)}, f32[1024,1024]{1,0:T(8,128)}) async-done(((f32[1024,1024]{1,0:T(8,128)}, f32[1024,1024]{1,0:T(8,128)}), (f32[1024,1024]{1,0:T(8,128)}, f32[1024,1024]{1,0:T(8,128)})) %all-reduce.3.cloned.1.call-update) | async-done | bytes 8388624 | tf_op jit(solution)/shard_map/psum | solution.py:58
  229.2 8.9 %broadcast_multiply_fusion = (f32[1024,1024]{1,0:T(8,128)}, f32[1024,1024]{1,0:T(8,128)}) fusion(f32[1024,1024]{1,0:T(8,128)} %get-tuple-element.13, f32[1024,1024]{1,0:T(8,128)} %get-tuple-element.12), kind=kLoop, calls=%fused_computation.2 | loop fusion | flops 2097152 | bytes 16777216 | tf_op jit(solution)/shard_map/mul | solution.py:60
  (4 shorter events, 0.0 us)
Async XLA Ops:
  10.4 30.5 %all-to-all-start = ((bf16[2,2,1024,128]{3,1,0,2:T(2,128)(2,1)}), bf16[2,2,1024,128]{3,1,0,2:T(2,128)(2,1)S(1)}, u32[]{:S(2)}, u32[]{:S(2)}) async-start(bf16[2,2,1024,128]{3,1,0,2:T(2,128)(2,1)} %copy.14), calls=%async_computation | async-start | bytes 2097152 | tf_op jit(solution)/shard_map/all_to_all | solution.py:53
  17.7 211.4 %all-reduce.3.cloned.1.call-start = ((), (), s32[]{:S(2)}) async-start(), calls=%async_computation.1 | async-start | bytes 16777216 | tf_op jit(solution)/shard_map/psum | solution.py:58
Sparse Core Ops, SparseCore 0:
  49.0 180.1 all-reduce.2
where the time goes:
time: 246 us; the launch traced here: 245 us
  waiting for transfers between devices  202 us (82%)
  between operations  14.1 us (6%)
  other arithmetic  8.99 us (4%)
  matrix products  7.62 us (3%)
  starting transfers between devices  7.35 us (3%)
  local copies, waits for them, and re-layouts  4.65 us (2%)
    psum x1, waiting for transfers between devices, local(): gram_real, gram_imag = lax.psum((shard_real, shard_imag), ('shift', 'row'))  180 us
    all_to_all x1, waiting for transfers between devices, local(): lax.all_to_all(solutions, 'shift', split_axis=2, concat_axis=0, tiled=True)  22.6 us
    mul x1, other arithmetic, local(): return (moments, gram_real * factor, gram_imag * factor)  8.85 us
    all_to_all x1, starting transfers between devices, local(): lax.all_to_all(solutions, 'shift', split_axis=2, concat_axis=0, tiled=True)  7.31 us
    dot_general x4, matrix products, pair_product(): jnp.einsum('krl,qrm->klqm', left, right, preferred_element_type=jnp.float32)  6.95 us
  transfers between devices with their start and end apart: 2, of which 2 were waited for; matrix products, arithmetic and copies ran while one was open for 0% of the time, Pallas kernels for 0%

commit v1 on v0

v1 whole, which is shorter than its diff:
```python
import functools
import math

import jax
import jax.numpy as jnp
import numpy as np
from jax import lax
from jax.experimental import pallas as pl
from jax.experimental.pallas import tpu as pltpu
from jax.sharding import PartitionSpec as P

PANELS = 8
PAIRS = PANELS * (PANELS // 2) + PANELS // 2
MESH = pl.DeviceIdType.MESH


def coefficients(all_shifts):
    indices = np.arange(all_shifts, dtype=np.float32)
    orders = np.arange(1, PANELS + 1, dtype=np.float32)
    step = (np.float32(2.0 * math.pi) * (indices + np.float32(0.5)) / np.float32(all_shifts)).astype(np.float32)
    angles = (orders[:, None] * step[None, :]).astype(np.float32).astype(np.float64)
    cos_part = np.cos(angles).astype(np.float32) / np.float32(all_shifts)
    sin_part = np.sin(angles).astype(np.float32) / np.float32(all_shifts)
    real_row = np.stack([cos_part, -sin_part], axis=-1)
    imag_row = np.stack([sin_part, cos_part], axis=-1)
    both = np.stack([real_row, imag_row], axis=0).reshape(-1)
    return both.astype(jnp.bfloat16).astype(np.float32)


def exchange(
    N, R, rows, T, factor,
    w_ref, x_ref, m_ref, ag, xs, acc, sbuf, gs, rs,
    a2a_s, a2a_r, sg_s, sg_r, rs_s, rs_r, ag_s, ag_r,
):
    X = N // 2
    Z = X // 2
    s = lax.axis_index("shift")
    r = lax.axis_index("row")
    core = lax.rem(s, 2)
    zx = s // 2
    z = zx // 2
    x = lax.rem(zx, 2)
    p = r * 2 + core
    inputs = x_ref.shape[0]
    outs = 2 * PANELS

    def remote(src, dst, ss, rr, to_s, to_r):
        return pltpu.make_async_remote_copy(
            src_ref=src, dst_ref=dst, send_sem=ss, recv_sem=rr,
            device_id={"shift": to_s, "row": to_r}, device_id_type=MESH,
        )

    partner = zx * 2 + 1 - core

    barrier = pltpu.get_barrier_semaphore()
    for i in range(1, N):
        pl.semaphore_signal(barrier, inc=1, device_id={"shift": lax.rem(s + i, N), "row": r}, device_id_type=MESH)
    for i in range(1, R):
        pl.semaphore_signal(barrier, inc=1, device_id={"shift": s, "row": lax.rem(r + i, R)}, device_id_type=MESH)
    pl.semaphore_wait(barrier, N - 1 + R - 1)

    def a2a(i):
        to = lax.rem(s + i, N)
        return remote(
            x_ref.at[:, pl.ds(pl.multiple_of(to * rows, rows), rows), :], xs.at[i],
            a2a_s.at[i], a2a_r.at[i], to, r,
        )

    def order(j):
        return 1 + lax.rem(N // 2 - 1 + j, N - 1)

    def send_one(j, c):
        a2a(order(j)).start()
        return c

    lax.fori_loop(0, N - 1, send_one, 0)

    strip = 16 if rows % 16 == 0 else rows

    def weigh(block, source, first):
        for b in range(rows // strip):
            at = slice(b * strip, (b + 1) * strip)
            parts = [block(c, at).astype(jnp.float32) for c in range(inputs)]
            for o in range(outs):
                base = o * inputs * N + source * inputs
                total = parts[0] * w_ref[base]
                for c in range(1, inputs):
                    total += parts[c] * w_ref[base + c]
                if first:
                    acc[o, at, :] = total
                else:
                    acc[o, at, :] += total

    weigh(lambda c, at: x_ref[c, pl.ds(pl.multiple_of(s * rows + at.start, strip), strip), :], s, True)

    def take_one(j, c):
        i = order(j)
        a2a(i).wait_recv()
        weigh(lambda q, at: xs[i, q, at, :], lax.rem(s - i + N, N), False)
        return c

    lax.fori_loop(0, N - 1, take_one, 0)

    def round_one(o, c):
        value = acc[o].astype(jnp.bfloat16)
        sbuf[p, o] = value
        m_ref[o] = value
        return c

    lax.fori_loop(0, outs, round_one, 0)

    done = []

    def share(slot, sem, to_s, to_r):
        return remote(sbuf.at[slot], sbuf.at[slot], sg_s.at[sem], sg_r.at[slot], to_s, to_r)

    for i in range(1, R):
        c = share(p, i, s, lax.rem(r + i, R))
        c.start()
        done.append(c)
    c = share(p, 0, partner, r)
    c.start()
    done.append(c)
    for i in range(1, R):
        slot = lax.rem(r - i + R, R) * 2 + core
        share(slot, 0, s, r).wait_recv()
        c = share(slot, R - 1 + i, partner, r)
        c.start()
        done.append(c)
    for i in range(R):
        share(lax.rem(r + i, R) * 2 + 1 - core, 0, s, r).wait_recv()

    depth = 2 * R * rows

    def pair_one(t, c):
        u = jnp.minimum(p * T + t, PAIRS - 1)
        k = lax.rem(u, PANELS)
        q = lax.rem(k + u // PANELS, PANELS)
        lr = sbuf[:, k].reshape(depth, -1)
        li = sbuf[:, PANELS + k].reshape(depth, -1)
        rr = sbuf[:, q].reshape(depth, -1)
        ri = sbuf[:, PANELS + q].reshape(depth, -1)
        dims = (((0,), (0,)), ((), ()))
        out = lax.dot_general(
            lr, jnp.concatenate([rr, ri], axis=1), dims, preferred_element_type=jnp.float32
        ) + lax.dot_general(
            li, jnp.concatenate([ri, -rr], axis=1), dims, preferred_element_type=jnp.float32
        )
        out = (out * factor).astype(jnp.bfloat16)
        cut = out.shape[0] // X
        for m in range(X):
            gs[m, t] = out[m * cut : (m + 1) * cut]
        return c

    lax.fori_loop(0, T, pair_one, 0)

    def reduce(i):
        to = lax.rem(zx + i, X)
        return remote(gs.at[to], rs.at[i], rs_s.at[i], rs_r.at[i], to * 2 + core, r)

    for j in range(X - 1):
        i = 1 + (X // 2 - 1 + j) % (X - 1)
        c = reduce(i)
        c.start()
        done.append(c)
    for i in range(1, X):
        reduce(i).wait_recv()

    def sum_one(t, c):
        total = gs[zx, t].astype(jnp.float32)
        for i in range(1, X):
            total += rs[i, t].astype(jnp.float32)
        ag[p, zx, t] = total.astype(jnp.bfloat16)
        return c

    lax.fori_loop(0, T, sum_one, 0)

    count = [0]

    def forward(pp, at, to_s, to_r):
        c = remote(ag.at[pp, at], ag.at[pp, at], ag_s.at[count[0]], ag_r.at[pp, at], to_s, to_r)
        count[0] += 1
        c.start()
        done.append(c)

    def arrive(pp, at):
        remote(ag.at[pp, at], ag.at[pp, at], ag_s.at[0], ag_r.at[pp, at], s, r).wait_recv()

    def to_rows_and_partner(at):
        for i in range(1, R):
            forward(p, at, s, lax.rem(r + i, R))
        forward(p, at, partner, r)

    other_x = (z * 2 + 1 - x) * 2 + core
    for i in range(1, Z):
        forward(p, zx, (lax.rem(z + i, Z) * 2 + x) * 2 + core, r)
    forward(p, zx, other_x, r)
    to_rows_and_partner(zx)
    for i in range(1, Z):
        at = lax.rem(z - i + Z, Z) * 2 + x
        arrive(p, at)
        forward(p, at, other_x, r)
        to_rows_and_partner(at)
    for i in range(Z):
        at = lax.rem(z - i + Z, Z) * 2 + 1 - x
        arrive(p, at)
        to_rows_and_partner(at)
    sequence = [lax.rem(z - i + Z, Z) * 2 + x for i in range(Z)]
    sequence += [lax.rem(z - i + Z, Z) * 2 + 1 - x for i in range(Z)]
    for at in sequence:
        for i in range(1, R):
            pp = lax.rem(r - i + R, R) * 2 + core
            arrive(pp, at)
            forward(pp, at, partner, r)
    for at in sequence:
        for i in range(R):
            arrive(lax.rem(r + i, R) * 2 + 1 - core, at)

    def drain(j, c):
        a2a(order(j)).wait_send()
        return c

    lax.fori_loop(0, N - 1, drain, 0)
    for c in done:
        c.wait_send()


def expand(T, ag_ref, re_ref, im_ref):
    k = pl.program_id(0)
    width = re_ref.shape[0]

    def pair(u):
        return ag_ref[u // T, :, lax.rem(u, T)].astype(jnp.float32).reshape(width, 2 * width)

    half = PANELS // 2
    for d in range(PANELS):
        q = lax.rem(k + d, PANELS)
        at = pl.ds(pl.multiple_of(q * width, width), width)
        if d < half:
            v = pair(PANELS * d + k)
            re, im = v[:, :width], v[:, width:]
        elif d == half:
            v = pair(PANELS * half + jnp.minimum(k, q))
            re, im = v[:, :width], v[:, width:]
            re, im = jnp.where(k < half, re, re.T), jnp.where(k < half, im, -im.T)
        else:
            v = pair(PANELS * (PANELS - d) + q)
            re, im = v[:, :width].T, -v[:, width:].T
        re_ref[:, at] = re
        im_ref[:, at] = im


def local(N, R, solutions):
    shifts, parts, height, width = solutions.shape
    rows = height // N
    X = N // 2
    Z = X // 2
    G = 2 * R
    T = -(-PAIRS // G)
    cut = width // X
    inputs = shifts * parts
    outs = 2 * PANELS
    factor = 1.0 / math.sqrt(height * R)
    w = jnp.asarray(coefficients(shifts * N))
    bf, dma = jnp.bfloat16, pltpu.SemaphoreType.DMA
    sends = (Z - 1) + Z + X * R + R * X
    vmem = pl.BlockSpec(memory_space=pltpu.VMEM)
    moments, parts_of_gram = pl.pallas_call(
        functools.partial(exchange, N, R, rows, T, factor),
        out_shape=(
            jax.ShapeDtypeStruct((outs, rows, width), bf),
            jax.ShapeDtypeStruct((G, X, T, cut, 2 * width), bf),
        ),
        in_specs=[pl.BlockSpec(memory_space=pltpu.SMEM), vmem],
        out_specs=(vmem, vmem),
        scratch_shapes=[
            pltpu.VMEM((N, inputs, rows, width), bf),
            pltpu.VMEM((outs, rows, width), jnp.float32),
            pltpu.VMEM((G, outs, rows, width), bf),
            pltpu.VMEM((X, T, cut, 2 * width), bf),
            pltpu.VMEM((X, T, cut, 2 * width), bf),
            dma((N,)), dma((N,)), dma((2 * R,)), dma((G,)),
            dma((X,)), dma((X,)), dma((sends,)), dma((G, X)),
        ],
        compiler_params=pltpu.CompilerParams(
            collective_id=0, has_side_effects=True, vmem_limit_bytes=40 * 2**20
        ),
        cost_estimate=pl.CostEstimate(flops=10**9, bytes_accessed=2**23, transcendentals=0),
    )(w, solutions.reshape(inputs, height, width))
    size = PANELS * width
    block = pl.BlockSpec((width, size), lambda k: (k, 0))
    gram_real, gram_imag = pl.pallas_call(
        functools.partial(expand, T),
        grid=(PANELS,),
        out_shape=(jax.ShapeDtypeStruct((size, size), jnp.float32),) * 2,
        in_specs=[vmem],
        out_specs=(block, block),
        cost_estimate=pl.CostEstimate(flops=10**7, bytes_accessed=2**24, transcendentals=0),
    )(parts_of_gram)
    return moments.reshape(2, PANELS, rows, width), gram_real, gram_imag


def solution(mesh):
    return jax.shard_map(
        functools.partial(local, mesh.shape["shift"], mesh.shape["row"]),
        mesh=mesh,
        in_specs=(P("shift", None, "row", None),),
        out_specs=(P(None, None, ("row", "shift"), None), P(), P()),
        check_vma=False,
    )
```

time: 246 us -> 87 us (0.35)
  waiting for transfers between devices: 202 us -> 0 us
  Pallas kernels: 0 us -> 82.1 us
  between operations: 14.1 us -> 0.66 us
  other arithmetic: 8.99 us -> 0 us
  matrix products: 7.62 us -> 0 us
  starting transfers between devices: 7.35 us -> 0 us
    psum x1 -> x0, waiting for transfers between devices: 180 us -> none  [local(): gram_real, gram_imag = lax.psum((shard_real, shard_imag), ('shift', 'row'))]
    pallas_call x0 -> x2, Pallas kernels: none -> 82.1 us  [the longest x1 75.4 us: local(): pl.pallas_call(functools.partial(exchange, N, R, rows, T, factor), out_sh...]
    all_to_all x1 -> x0, waiting for transfers between devices: 22.6 us -> none  [local(): lax.all_to_all(solutions, 'shift', split_axis=2, concat_axis=0, tiled=True)]
    mul x1 -> x0, other arithmetic: 8.85 us -> none  [local(): return (moments, gram_real * factor, gram_imag * factor)]
    dot_general x5 -> x0, matrix products: 7.62 us -> none  [the longest x4 6.95 us: pair_product(): jnp.einsum('krl,qrm->klqm', left, right, preferred_element_type=jnp.float32)]
    all_to_all x1 -> x0, starting transfers between devices: 7.31 us -> none  [local(): lax.all_to_all(solutions, 'shift', split_axis=2, concat_axis=0, tiled=True)]
  transfers between devices with their start and end apart: 2 -> 0, of which waited for: 2 -> 0; matrix products, arithmetic and copies ran while one was open for 0% -> 0% of each run, Pallas kernels for 0% -> 0%
where the time goes in v1:
time: 87 us; the launch traced here: 86.8 us
  Pallas kernels  82.1 us (94%)
  local copies, waits for them, and re-layouts  4.02 us (5%)
    pallas_call x1, Pallas kernels, local(): pl.pallas_call(functools.partial(exchange, N, R, rows, T, factor), out_sh...  75.4 us
    pallas_call x1, Pallas kernels, local(): pl.pallas_call(functools.partial(expand, T), grid=(PANELS,), out_shape=(j...  6.74 us
    unnamed x7, local copies, waits for them, and re-layouts  4.02 us

profile of v1, /device:TPU:1, one launch (start us, length us, event | category | flops | bytes accessed | tf_op | source)
XLA Modules:
  0.0 86.8 jit_solution(2298438373953568305)
XLA Ops:
  0.6 0.0 copy-start.1
  0.6 1.2 %copy-done.1 = bf16[2,2,1024,128]{3,2,1,0:T(8,128)(2,1)S(1)} copy-done((bf16[2,2,1024,128]{3,2,1,0:T(8,128)(2,1)S(1)}, bf16[2,2,1024,128]{3,2,1,0:T(8,128)(2,1)}, u32[]{:S(2)}) %copy-start.1) | copy-done | bytes 1048600
  1.9 0.0 copy-start.2
  1.9 0.7 copy-done.2
  2.5 75.4 %shard_map.49 = (bf16[16,64,128]{2,1,0:T(8,128)(2,1)S(1)}, bf16[4,8,9,16,256]{4,3,2,1,0:T(8,128)(2,1)S(1)}) custom-call(f32[1024]{0:T(1024)S(1)} %copy-done.2, bf16[4,1024,128]{2,1,0:T(8,128)(2,1)S(1)} %bitcast.3), custom_call_target="tpu_custom_call" | custom-call | flops 1000000000 | bytes 8388608 | tf_op jit(solution)/shard_map/pallas_call | solution.py:268
  77.9 0.0 copy-start
  77.9 1.4 %copy-done = bf16[4,8,9,16,256]{4,3,2,1,0:T(8,128)(2,1)} copy-done((bf16[4,8,9,16,256]{4,3,2,1,0:T(8,128)(2,1)}, bf16[4,8,9,16,256]{4,3,2,1,0:T(8,128)(2,1)S(1)}, u32[]{:S(2)}) %copy-start) | copy-done | bytes 2359320
  79.4 6.7 %shard_map.50 = (f32[1024,1024]{1,0:T(8,128)}, f32[1024,1024]{1,0:T(8,128)}) custom-call(bf16[4,8,9,16,256]{4,3,2,1,0:T(8,128)(2,1)} %copy-done), custom_call_target="tpu_custom_call" | custom-call | flops 10000000 | bytes 16777216 | tf_op jit(solution)/shard_map/pallas_call | solution.py:292
  86.1 0.7 copy.6
Async XLA Ops:
  0.6 1.2 %copy-start.1 = (bf16[2,2,1024,128]{3,2,1,0:T(8,128)(2,1)S(1)}, bf16[2,2,1024,128]{3,2,1,0:T(8,128)(2,1)}, u32[]{:S(2)}) copy-start(bf16[2,2,1024,128]{3,2,1,0:T(8,128)(2,1)} %param.2) | copy-start | bytes 3145732
  1.9 0.7 copy-start.2
  77.9 1.4 %copy-start = (bf16[4,8,9,16,256]{4,3,2,1,0:T(8,128)(2,1)}, bf16[4,8,9,16,256]{4,3,2,1,0:T(8,128)(2,1)S(1)}, u32[]{:S(2)}) copy-start(bf16[4,8,9,16,256]{4,3,2,1,0:T(8,128)(2,1)S(1)} %get-tuple-element.8.ag_ref) | copy-start | bytes 7077892

commit v2 on v1

v2 whole, which is shorter than its diff:
```python
import functools
import math

import jax
import jax.numpy as jnp
import numpy as np
from jax import lax
from jax.experimental import pallas as pl
from jax.experimental.pallas import tpu as pltpu
from jax.sharding import PartitionSpec as P

PANELS = 8
PAIRS = PANELS * (PANELS // 2) + PANELS // 2
UNITS = 2 * PAIRS
HALVES = 2
MESH = pl.DeviceIdType.MESH


def coefficients(all_shifts):
    indices = np.arange(all_shifts, dtype=np.float32)
    orders = np.arange(1, PANELS + 1, dtype=np.float32)
    step = (np.float32(2.0 * math.pi) * (indices + np.float32(0.5)) / np.float32(all_shifts)).astype(np.float32)
    angles = (orders[:, None] * step[None, :]).astype(np.float32).astype(np.float64)
    cos_part = np.cos(angles).astype(np.float32) / np.float32(all_shifts)
    sin_part = np.sin(angles).astype(np.float32) / np.float32(all_shifts)
    real_row = np.stack([cos_part, -sin_part], axis=-1)
    imag_row = np.stack([sin_part, cos_part], axis=-1)
    both = np.stack([real_row, imag_row], axis=0).reshape(-1)
    return both.astype(jnp.bfloat16).astype(np.float32)


def exchange(
    N, R, rows, T, factor,
    w_ref, x_ref, m_ref, ag, xs, acc, sbuf, gs, rs,
    a2a_s, a2a_r, sg_s, sg_r, rs_s, rs_r, ag_s, ag_r,
):
    Z = N // 4
    s = lax.axis_index("shift")
    r = lax.axis_index("row")
    core = lax.rem(s, 2)
    z = s // 4
    x = lax.rem(s // 2, 2)
    inputs = x_ref.shape[0]
    outs = 2 * PANELS
    part = rows // HALVES

    def member(x_, r_, c_):
        return (r_ * 2 + x_) * 2 + c_

    def place(z_, x_, c_):
        return (z_ * 2 + x_) * 2 + c_

    p = member(x, r, core)
    partner = place(z, x, 1 - core)
    across = place(z, 1 - x, core)

    def row_at(i):
        return lax.rem(r + i + R, R)

    def remote(src, dst, ss, rr, to_s, to_r):
        return pltpu.make_async_remote_copy(
            src_ref=src, dst_ref=dst, send_sem=ss, recv_sem=rr,
            device_id={"shift": to_s, "row": to_r}, device_id_type=MESH,
        )

    barrier = pltpu.get_barrier_semaphore()
    for i in range(1, N):
        pl.semaphore_signal(barrier, inc=1, device_id={"shift": lax.rem(s + i, N), "row": r}, device_id_type=MESH)
    for i in range(1, R):
        pl.semaphore_signal(barrier, inc=1, device_id={"shift": s, "row": row_at(i)}, device_id_type=MESH)
    pl.semaphore_wait(barrier, N - 1 + R - 1)

    def a2a(h, i):
        to = lax.rem(s + i, N)
        return remote(
            x_ref.at[:, pl.ds(pl.multiple_of(to * rows + h * part, part), part), :], xs.at[h, i],
            a2a_s.at[h, i], a2a_r.at[h, i], to, r,
        )

    def order(j):
        return 1 + lax.rem(N // 2 - 1 + j, N - 1)

    def send_one(j, c):
        a2a(j // (N - 1), order(lax.rem(j, N - 1))).start()
        return c

    lax.fori_loop(0, HALVES * (N - 1), send_one, 0)

    strip = 16 if part % 16 == 0 else part

    def weigh(block, source, first):
        for b in range(part // strip):
            at = slice(b * strip, (b + 1) * strip)
            parts = [block(c, at).astype(jnp.float32) for c in range(inputs)]
            for o in range(outs):
                base = o * inputs * N + source * inputs
                total = parts[0] * w_ref[base]
                for c in range(1, inputs):
                    total += parts[c] * w_ref[base + c]
                if first:
                    acc[o, at, :] = total
                else:
                    acc[o, at, :] += total

    def take(h, low, high):
        def take_one(j, c):
            i = order(j)
            a2a(h, i).wait_recv()
            weigh(lambda q, at: xs[h, i, q, at, :], lax.rem(s - i + N, N), False)
            return c

        lax.fori_loop(low, high, take_one, 0)

    def own(h):
        weigh(
            lambda c, at: x_ref[c, pl.ds(pl.multiple_of(s * rows + h * part + at.start, strip), strip), :],
            s, True,
        )

    def round_all(h):
        def round_one(o, c):
            value = acc[o].astype(jnp.bfloat16)
            sbuf[h, p, o] = value
            m_ref[o, h * part : (h + 1) * part, :] = value
            return c

        lax.fori_loop(0, outs, round_one, 0)

    done = []

    def spreader(view, send_sems, recv_sems):
        count = [0]

        def copy(at, slot, to_s, to_r):
            return remote(view(at, slot), view(at, slot), send_sems.at[count[0]], recv_sems.at[at, slot], to_s, to_r)

        def forward(at, slot, to_s, to_r):
            c = copy(at, slot, to_s, to_r)
            count[0] += 1
            c.start()
            done.append(c)

        def arrive(at, slot):
            remote(view(at, slot), view(at, slot), send_sems.at[0], recv_sems.at[at, slot], s, r).wait_recv()

        def spread(at):
            forward(at, p, across, r)
            for i in range(1, R):
                forward(at, p, s, row_at(i))
            forward(at, p, partner, r)

        def relay(at):
            arrive(at, member(1 - x, r, core))
            for i in range(1, R):
                arrive(at, member(x, row_at(-i), core))
            for i in range(1, R):
                first = core == 0
                slot = jnp.where(first, member(1 - x, r, core), member(x, row_at(-i), core))
                forward(at, slot, jnp.where(first, s, across), jnp.where(first, row_at(i), r))
            forward(at, member(1 - x, r, core), partner, r)
            for i in range(1, R):
                forward(at, member(x, row_at(-i), core), partner, r)

        def diagonal(at):
            for i in range(1, R):
                slot = member(1 - x, row_at(-i), core)
                arrive(at, slot)
                forward(at, slot, partner, r)

        def rest(at):
            for i in range(R):
                for o in range(2):
                    arrive(at, member(lax.rem(x + o, 2), row_at(i), 1 - core))

        return spread, relay, diagonal, rest, arrive, forward

    spread, relay, diagonal, rest, _, _ = spreader(lambda h, slot: sbuf.at[h, slot], sg_s, sg_r)
    for h in range(HALVES):
        own(h)
        if h == 0:
            take(h, 0, N - 1)
        else:
            mid = (2 * (N - 1)) // 3
            take(h, 0, mid)
            relay(h - 1)
            take(h, mid, N - 1)
        round_all(h)
        spread(h)
        if h > 0:
            diagonal(h - 1)
    relay(HALVES - 1)
    diagonal(HALVES - 1)
    for h in range(HALVES):
        rest(h)

    depth = 4 * R * rows
    first_pair = (p * T) // 2
    odd = lax.rem(p * T, 2)

    def pair_one(j, c):
        u = jnp.minimum(first_pair + j, PAIRS - 1)
        k = lax.rem(u, PANELS)
        q = lax.rem(k + u // PANELS, PANELS)
        lr = sbuf[:, :, k].reshape(depth, -1)
        li = sbuf[:, :, PANELS + k].reshape(depth, -1)
        rr = sbuf[:, :, q].reshape(depth, -1)
        ri = sbuf[:, :, PANELS + q].reshape(depth, -1)
        dims = (((0,), (0,)), ((), ()))
        out = lax.dot_general(
            lr, jnp.concatenate([rr, ri], axis=1), dims, preferred_element_type=jnp.float32
        ) + lax.dot_general(
            li, jnp.concatenate([ri, -rr], axis=1), dims, preferred_element_type=jnp.float32
        )
        out = (out * factor).astype(jnp.bfloat16)
        cut = out.shape[0] // (2 * Z)
        for half in range(2):
            for m in range(Z):
                n = half * Z + m
                gs[m, 2 * j + half + 1 - odd] = out[n * cut : (n + 1) * cut]
        return c

    lax.fori_loop(0, (T + 2) // 2 if T % 2 else T // 2, pair_one, 0)

    def reduce(i):
        to = lax.rem(z + i, Z)
        return remote(gs.at[to, pl.ds(1, T)], rs.at[i], rs_s.at[i], rs_r.at[i], place(to, x, core), r)

    for j in range(Z - 1):
        c = reduce(1 + (Z // 2 - 1 + j) % (Z - 1))
        c.start()
        done.append(c)
    for i in range(1, Z):
        reduce(i).wait_recv()

    def sum_one(t, c):
        total = gs[z, t + 1].astype(jnp.float32)
        for i in range(1, Z):
            total += rs[i, t].astype(jnp.float32)
        ag[p, z, t] = total.astype(jnp.bfloat16)
        return c

    lax.fori_loop(0, T, sum_one, 0)

    spread, relay, diagonal, rest, arrive, forward = spreader(lambda at, slot: ag.at[slot, at], ag_s, ag_r)
    for j in range(Z - 1):
        i = 1 + (Z // 2 - 1 + j) % (Z - 1)
        forward(z, p, place(lax.rem(z + i, Z), x, core), r)
    ats = [lax.rem(z + Z - i, Z) for i in range(Z)]
    for n in range(Z + 2):
        if n < Z:
            if n > 0:
                arrive(ats[n], p)
            spread(ats[n])
        if 0 <= n - 1 < Z:
            relay(ats[n - 1])
        if 0 <= n - 2 < Z:
            diagonal(ats[n - 2])
    for at in ats:
        rest(at)

    def drain(j, c):
        a2a(j // (N - 1), order(lax.rem(j, N - 1))).wait_send()
        return c

    lax.fori_loop(0, HALVES * (N - 1), drain, 0)
    for c in done:
        c.wait_send()


def expand(T, m_in, ag_ref, m_out, re_out, im_out, re_buf, im_buf, sems, m_sem):
    width = re_buf.shape[1]
    half = PANELS // 2
    keep = pltpu.make_async_copy(m_in, m_out, m_sem)
    keep.start()

    def unit(n):
        return ag_ref[n // T, :, lax.rem(n, T)].astype(jnp.float32).reshape(width // 2, 2 * width)

    def pair(u):
        return jnp.concatenate([unit(2 * u), unit(2 * u + 1)], axis=0)

    def writes(k, slot):
        at = pl.ds(pl.multiple_of(k * width, width), width)
        return (
            pltpu.make_async_copy(re_buf.at[k], re_out.at[at], sems.at[0, k]),
            pltpu.make_async_copy(im_buf.at[k], im_out.at[at], sems.at[1, k]),
        )

    def one(k, c):
        for d in range(PANELS):
            q = lax.rem(k + d, PANELS)
            at = pl.ds(pl.multiple_of(q * width, width), width)
            if d < half:
                v = pair(PANELS * d + k)
                re, im = v[:, :width], v[:, width:]
            elif d == half:
                v = pair(PANELS * half + jnp.minimum(k, q))
                re, im = v[:, :width], v[:, width:]
                re, im = jnp.where(k < half, re, re.T), jnp.where(k < half, im, -im.T)
            else:
                v = pair(PANELS * (PANELS - d) + q)
                re, im = v[:, :width].T, -v[:, width:].T
            re_buf[k, :, at] = re
            im_buf[k, :, at] = im
        for copy in writes(k, k):
            copy.start()
        return c

    lax.fori_loop(0, PANELS, one, 0)

    def finish(k, c):
        for copy in writes(k, k):
            copy.wait()
        return c

    lax.fori_loop(0, PANELS, finish, 0)
    keep.wait()


def local(N, R, solutions):
    shifts, parts, height, width = solutions.shape
    rows = height // N
    Z = N // 4
    G = 4 * R
    T = -(-UNITS // G)
    cut = width // (2 * Z)
    inputs = shifts * parts
    outs = 2 * PANELS
    part = rows // HALVES
    factor = 1.0 / math.sqrt(height * R)
    w = jnp.asarray(coefficients(shifts * N))
    bf, dma = jnp.bfloat16, pltpu.SemaphoreType.DMA
    shared = 4 * R
    vmem = pl.BlockSpec(memory_space=pltpu.VMEM)
    moments, parts_of_gram = pl.pallas_call(
        functools.partial(exchange, N, R, rows, T, factor),
        out_shape=(
            jax.ShapeDtypeStruct((outs, rows, width), bf),
            jax.ShapeDtypeStruct((G, Z, T, cut, 2 * width), bf),
        ),
        in_specs=[pl.BlockSpec(memory_space=pltpu.SMEM), vmem],
        out_specs=(vmem, vmem),
        scratch_shapes=[
            pltpu.VMEM((HALVES, N, inputs, part, width), bf),
            pltpu.VMEM((outs, part, width), jnp.float32),
            pltpu.VMEM((HALVES, G, outs, part, width), bf),
            pltpu.VMEM((Z, T + 2, cut, 2 * width), bf),
            pltpu.VMEM((Z, T, cut, 2 * width), bf),
            dma((HALVES, N)), dma((HALVES, N)), dma((HALVES * shared,)), dma((HALVES, G)),
            dma((Z,)), dma((Z,)), dma((Z * shared + Z,)), dma((Z, G)),
        ],
        compiler_params=pltpu.CompilerParams(
            collective_id=0, has_side_effects=True, vmem_limit_bytes=32 * 2**20
        ),
        cost_estimate=pl.CostEstimate(flops=10**9, bytes_accessed=2**23, transcendentals=0),
    )(w, solutions.reshape(inputs, height, width))
    size = PANELS * width
    anywhere = pl.BlockSpec(memory_space=pl.ANY)
    moments, gram_real, gram_imag = pl.pallas_call(
        functools.partial(expand, T),
        out_shape=(
            jax.ShapeDtypeStruct((outs, rows, width), bf),
            jax.ShapeDtypeStruct((size, size), jnp.float32),
            jax.ShapeDtypeStruct((size, size), jnp.float32),
        ),
        in_specs=[vmem, vmem],
        out_specs=(anywhere, anywhere, anywhere),
        scratch_shapes=[
            pltpu.VMEM((PANELS, width, size), jnp.float32),
            pltpu.VMEM((PANELS, width, size), jnp.float32),
            dma((2, PANELS)),
            dma,
        ],
        compiler_params=pltpu.CompilerParams(vmem_limit_bytes=32 * 2**20),
        cost_estimate=pl.CostEstimate(flops=10**7, bytes_accessed=2**24, transcendentals=0),
    )(moments, parts_of_gram)
    return moments.reshape(2, PANELS, rows, width), gram_real, gram_imag


def solution(mesh):
    return jax.shard_map(
        functools.partial(local, mesh.shape["shift"], mesh.shape["row"]),
        mesh=mesh,
        in_specs=(P("shift", None, "row", None),),
        out_specs=(P(None, None, ("row", "shift"), None), P(), P()),
        check_vma=False,
    )
```

time: 87 us -> 79.2 us (0.910)
  Pallas kernels: 82.1 us -> 76.4 us
  local copies, waits for them, and re-layouts: 4.02 us -> 1.9 us
    pallas_call x1, Pallas kernels: 6.74 us -> 3.67 us  [local(): pl.pallas_call(functools.partial(expand, T), out_shape=(jax.ShapeDtypeStr...]
    pallas_call x1, Pallas kernels: 75.4 us -> 72.7 us  [local(): pl.pallas_call(functools.partial(exchange, N, R, rows, T, factor), out_sh...]
    unnamed x7 -> x4, local copies, waits for them, and re-layouts: 4.02 us -> 1.9 us
where the time goes in v2:
time: 79.2 us; the launch traced here: 79 us
  Pallas kernels  76.4 us (96%)
  local copies, waits for them, and re-layouts  1.9 us (2%)
    pallas_call x1, Pallas kernels, local(): pl.pallas_call(functools.partial(exchange, N, R, rows, T, factor), out_sh...  72.7 us
    pallas_call x1, Pallas kernels, local(): pl.pallas_call(functools.partial(expand, T), out_shape=(jax.ShapeDtypeStr...  3.67 us
    unnamed x4, local copies, waits for them, and re-layouts  1.9 us

profile of v2, /device:TPU:1, one launch (start us, length us, event | category | flops | bytes accessed | tf_op | source)
XLA Modules:
  0.0 79.0 jit_solution(17588606326020149250)
XLA Ops:
  0.6 0.0 copy-start
  0.6 1.2 %copy-done = bf16[2,2,1024,128]{3,2,1,0:T(8,128)(2,1)S(1)} copy-done((bf16[2,2,1024,128]{3,2,1,0:T(8,128)(2,1)S(1)}, bf16[2,2,1024,128]{3,2,1,0:T(8,128)(2,1)}, u32[]{:S(2)}) %copy-start) | copy-done | bytes 1048600
  1.9 0.0 copy-start.1
  1.9 0.7 copy-done.1
  2.5 72.7 %shard_map.49 = (bf16[16,64,128]{2,1,0:T(8,128)(2,1)S(1)}, bf16[8,4,9,16,256]{4,3,2,1,0:T(8,128)(2,1)S(1)}) custom-call(f32[1024]{0:T(1024)S(1)} %copy-done.1, bf16[4,1024,128]{2,1,0:T(8,128)(2,1)S(1)} %bitcast.2), custom_call_target="tpu_custom_call" | custom-call | flops 1000000000 | bytes 8388608 | tf_op jit(solution)/shard_map/pallas_call | solution.py:335
  75.3 3.7 %shard_map.50 = (bf16[16,64,128]{2,1,0:T(8,128)(2,1)}, f32[1024,1024]{1,0:T(8,128)}, f32[1024,1024]{1,0:T(8,128)}) custom-call(bf16[16,64,128]{2,1,0:T(8,128)(2,1)S(1)} %get-tuple-element.8.m_in, bf16[8,4,9,16,256]{4,3,2,1,0:T(8,128)(2,1)S(1)} %get-tuple-element.9.ag_ref), custom_call_target="tpu_custom_call" | custom-call | flops 10000000 | bytes 16777216 | tf_op jit(solution)/shard_map/pallas_call | solution.py:359
Async XLA Ops:
  0.6 1.2 %copy-start = (bf16[2,2,1024,128]{3,2,1,0:T(8,128)(2,1)S(1)}, bf16[2,2,1024,128]{3,2,1,0:T(8,128)(2,1)}, u32[]{:S(2)}) copy-start(bf16[2,2,1024,128]{3,2,1,0:T(8,128)(2,1)} %param.2) | copy-start | bytes 3145732
  1.9 0.7 copy-start.1

commit v3 on v2

--- a/solution.py
+++ b/solution.py
@@ -78,7 +78,7 @@
         )
 
     def order(j):
-        return 1 + lax.rem(N // 2 - 1 + j, N - 1)
+        return 1 + j
 
     def send_one(j, c):
         a2a(j // (N - 1), order(lax.rem(j, N - 1))).start()
@@ -242,10 +242,18 @@
     lax.fori_loop(0, T, sum_one, 0)
 
     spread, relay, diagonal, rest, arrive, forward = spreader(lambda at, slot: ag.at[slot, at], ag_s, ag_r)
-    for j in range(Z - 1):
-        i = 1 + (Z // 2 - 1 + j) % (Z - 1)
-        forward(z, p, place(lax.rem(z + i, Z), x, core), r)
-    ats = [lax.rem(z + Z - i, Z) for i in range(Z)]
+    def mate(m):
+        if Z & (Z - 1):
+            return lax.rem(z + m, Z), lax.rem(z + Z - m, Z)
+        out = z
+        for b in range(m.bit_length()):
+            if m >> b & 1:
+                out = out + (1 - 2 * lax.rem(z // (1 << b), 2)) * (1 << b)
+        return out, out
+
+    for m in range(1, Z):
+        forward(z, p, place(mate(m)[0], x, core), r)
+    ats = [z] + [mate(m)[1] for m in range(1, Z)]
     for n in range(Z + 2):
         if n < Z:
             if n > 0:

time: 79.2 us -> 76.2 us (0.962)
  Pallas kernels: 76.4 us -> 73.4 us
    pallas_call x1, Pallas kernels: 72.7 us -> 69.8 us  [local(): pl.pallas_call(functools.partial(exchange, N, R, rows, T, factor), out_sh...]
where the time goes in v3:
time: 76.2 us; the launch traced here: 76 us
  Pallas kernels  73.4 us (96%)
  local copies, waits for them, and re-layouts  1.9 us (2%)
    pallas_call x1, Pallas kernels, local(): pl.pallas_call(functools.partial(exchange, N, R, rows, T, factor), out_sh...  69.8 us
    pallas_call x1, Pallas kernels, local(): pl.pallas_call(functools.partial(expand, T), out_shape=(jax.ShapeDtypeStr...  3.67 us
    unnamed x4, local copies, waits for them, and re-layouts  1.9 us

profile of v3, /device:TPU:1, one launch (start us, length us, event | category | flops | bytes accessed | tf_op | source)
XLA Modules:
  0.0 76.0 jit_solution(9819543015635131897)
XLA Ops:
  0.6 0.0 copy-start
  0.6 1.2 %copy-done = bf16[2,2,1024,128]{3,2,1,0:T(8,128)(2,1)S(1)} copy-done((bf16[2,2,1024,128]{3,2,1,0:T(8,128)(2,1)S(1)}, bf16[2,2,1024,128]{3,2,1,0:T(8,128)(2,1)}, u32[]{:S(2)}) %copy-start) | copy-done | bytes 1048600
  1.9 0.0 copy-start.1
  1.9 0.7 copy-done.1
  2.5 69.8 %shard_map.49 = (bf16[16,64,128]{2,1,0:T(8,128)(2,1)S(1)}, bf16[8,4,9,16,256]{4,3,2,1,0:T(8,128)(2,1)S(1)}) custom-call(f32[1024]{0:T(1024)S(1)} %copy-done.1, bf16[4,1024,128]{2,1,0:T(8,128)(2,1)S(1)} %bitcast.2), custom_call_target="tpu_custom_call" | custom-call | flops 1000000000 | bytes 8388608 | tf_op jit(solution)/shard_map/pallas_call | solution.py:343
  72.3 3.7 %shard_map.50 = (bf16[16,64,128]{2,1,0:T(8,128)(2,1)}, f32[1024,1024]{1,0:T(8,128)}, f32[1024,1024]{1,0:T(8,128)}) custom-call(bf16[16,64,128]{2,1,0:T(8,128)(2,1)S(1)} %get-tuple-element.8.m_in, bf16[8,4,9,16,256]{4,3,2,1,0:T(8,128)(2,1)S(1)} %get-tuple-element.9.ag_ref), custom_call_target="tpu_custom_call" | custom-call | flops 10000000 | bytes 16777216 | tf_op jit(solution)/shard_map/pallas_call | solution.py:367
Async XLA Ops:
  0.6 1.2 %copy-start = (bf16[2,2,1024,128]{3,2,1,0:T(8,128)(2,1)S(1)}, bf16[2,2,1024,128]{3,2,1,0:T(8,128)(2,1)}, u32[]{:S(2)}) copy-start(bf16[2,2,1024,128]{3,2,1,0:T(8,128)(2,1)} %param.2) | copy-start | bytes 3145732
  1.9 0.7 copy-start.1
